TPU v7x, 32 devices: a whole 2x2x4 slice. The times are simulated.
32 devices in a mesh: ctx: 4 (over y, x), tp: 8 (over z, core).
Axes of the slice: x: 2, y: 2, z: 4, core: 2. Of those that a mesh axis runs over, the one named last changes fastest.
Arguments:
- tokens: bfloat16 [2048, 4096], P(('ctx', 'tp')), may hold values from -16 to 16
- upstream: bfloat16 [2048, 4096], P('ctx', 'tp'), may hold values from -6 to 6
- w_query: bfloat16 [4096, 4096], P('ctx', 'tp')
- w_keyval: bfloat16 [4096, 2048], P('ctx', 'tp')
- positions: int32 [2048], replicated, may hold values from 0 to 2047, as said below
- documents: int32 [2048], replicated, may hold values from 0 to 3, never falling along the last dimension, each value on 1 to 1024 neighbouring positions
Outputs:
- token_grad: bfloat16 [2048, 4096], P(('ctx', 'tp'))
- query_grad: float32 [4096, 4096], P('ctx', 'tp')
- keyval_grad: float32 [4096, 2048], P('ctx', 'tp')
Inputs may be any that keep to these rules, and one draw needn't show every extreme that they name: Each stored run of 512 tokens holds consecutive increasing positions; the two runs of the tokens of one context rank are the blocks k and 7 - k of the sequence for some k; all runs together hold every position once.
All inputs are finite; a program needn't handle non-finite values.
Results may differ from a plain program's by a relative error of at most 0.02.
The roundings to bfloat16 on the way count: a program that leaves them out, or rounds other values in their place, can miss the bound.
Values may be sent and summed in bfloat16 or wider, within the bound.
No kernel may reach another device: no remote copies, remote signals or barrier semaphores. Data moves between devices by JAX's collectives and lax.ppermute only.
A program may use at most 128 MiB of HBM per device.

v0:
```python
import jax
import jax.numpy as jnp
from jax import lax
from jax.sharding import PartitionSpec as P

KEY_VALUE_HEADS = 8
HEAD_DIMENSION = 128
rope_base = 500000.0


def partner_2(block, axis, bit):
    count = lax.axis_size(axis)
    route = []
    for low in range(count):
        high = low | 1 << bit
        if high != low and high < count:
            route += [(low, high), (high, low)]
    return lax.ppermute(block, axis, route)


def rotation_tables(positions):
    half_width = HEAD_DIMENSION // 2
    frequency = rope_base ** (-(jnp.arange(half_width, dtype=jnp.float32) * 2.0 / HEAD_DIMENSION))
    angles = positions.astype(jnp.float32)[:, None] * frequency[None, :]
    cosine = jnp.concatenate([jnp.cos(angles), jnp.cos(angles)], axis=1)
    sine = jnp.concatenate([jnp.sin(angles), jnp.sin(angles)], axis=1)
    return (cosine, sine)


def rotate(values, cosine, sine):
    half_width = values.shape[-1] // 2
    turned = jnp.concatenate([-values[..., half_width:], values[..., :half_width]], axis=-1)
    return values * cosine[:, None, :] + turned * sine[:, None, :]


def rotate_back(gradient, cosine, sine):
    half_width = gradient.shape[-1] // 2
    scaled = gradient * sine[:, None, :]
    turned = jnp.concatenate([scaled[..., half_width:], -scaled[..., :half_width]], axis=-1)
    return gradient * cosine[:, None, :] + turned


def attend(
    query_rows, grad_out, keys_all, values_all, query_pos, query_doc, key_pos, key_doc, scaling
):
    f32 = jnp.float32
    tok_rows, head_count, head_width = query_rows.shape
    block_rows = min(tok_rows, 128)
    block_count = tok_rows // block_rows
    seq_len = keys_all.shape[0]

    def advance(totals, inputs):
        key_total, value_total = totals
        query_block, grad_block, pos_block, doc_block = inputs
        scores = (
            jnp.einsum("qhd,kd->hqk", query_block, keys_all, preferred_element_type=f32) * scaling
        )
        visible = (key_pos[None, :] <= pos_block[:, None]) & (
            key_doc[None, :] == doc_block[:, None]
        )
        scores = jnp.where(visible[None], scores, -1e30)
        row_peak = jnp.max(scores, axis=-1, keepdims=True)
        exponent = jnp.exp(scores - row_peak)
        probs = exponent / jnp.sum(exponent, axis=-1, keepdims=True)
        probs_half = probs.astype(jnp.bfloat16)
        output = jnp.einsum("hqk,kd->qhd", probs_half, values_all, preferred_element_type=f32)
        deltas = jnp.sum(grad_block.astype(f32) * output, axis=-1)
        prob_grad = jnp.einsum("qhd,kd->hqk", grad_block, values_all, preferred_element_type=f32)
        score_grad = (probs * (prob_grad - deltas.T[:, :, None])).astype(jnp.bfloat16)
        dquery = (
            jnp.einsum("hqk,kd->qhd", score_grad, keys_all, preferred_element_type=f32) * scaling
        )
        key_total = (
            key_total
            + jnp.einsum("hqk,qhd->kd", score_grad, query_block, preferred_element_type=f32)
            * scaling
        )
        value_total = value_total + jnp.einsum(
            "hqk,qhd->kd", probs_half, grad_block, preferred_element_type=f32
        )
        return ((key_total, value_total), dquery)

    blank_keys = jnp.zeros((seq_len, head_width), f32)
    inputs = (
        query_rows.reshape(block_count, block_rows, head_count, head_width),
        grad_out.reshape(block_count, block_rows, head_count, head_width),
        query_pos.reshape(block_count, block_rows),
        query_doc.reshape(block_count, block_rows),
    )
    (key_total, value_total), dquery = lax.scan(advance, (blank_keys, blank_keys), inputs)
    return (dquery.reshape(tok_rows, head_count, head_width), key_total, value_total)


def shards(tokens, upstream, w_query, w_keyval, positions, documents):
    f32 = jnp.float32
    ctx_rank = lax.axis_index("ctx")
    tp_rank = lax.axis_index("tp")
    tensor_split_count = lax.axis_size("tp")
    gathered = lax.all_gather(tokens, "tp", axis=0, tiled=True)
    tok_rows = gathered.shape[0]
    query_cols = w_query.shape[1]
    head_count = query_cols // HEAD_DIMENSION
    pairing_flags = (tensor_split_count // KEY_VALUE_HEADS).bit_length() - 1
    doc_all = jnp.take(documents, positions)
    cosine_all, sine_all = rotation_tables(positions)
    row_offset = ctx_rank * tok_rows
    my_pos = lax.dynamic_slice_in_dim(positions, row_offset, tok_rows, 0)
    my_doc = lax.dynamic_slice_in_dim(doc_all, row_offset, tok_rows, 0)
    my_cos = lax.dynamic_slice_in_dim(cosine_all, row_offset, tok_rows, 0)
    my_sin = lax.dynamic_slice_in_dim(sine_all, row_offset, tok_rows, 0)
    query_full, keyval_full = (
        lax.all_gather(w_query, "ctx", axis=0, tiled=True),
        lax.all_gather(w_keyval, "ctx", axis=0, tiled=True),
    )
    query_raw = jnp.dot(gathered, query_full, preferred_element_type=f32)
    keyval_raw = jnp.dot(gathered, keyval_full, preferred_element_type=f32)
    query_rot = rotate(
        query_raw.reshape(tok_rows, head_count, HEAD_DIMENSION), my_cos, my_sin
    ).astype(jnp.bfloat16)
    head_kv = keyval_raw.astype(jnp.bfloat16)
    for bit_index in range(pairing_flags):
        partner = partner_2(head_kv, "tp", bit_index)
        is_lower = tp_rank // (1 << bit_index) % 2 == 0
        head_kv = jnp.where(
            is_lower,
            jnp.concatenate([head_kv, partner], axis=1),
            jnp.concatenate([partner, head_kv], axis=1),
        )
    key_rot = rotate(head_kv[:, None, :HEAD_DIMENSION].astype(f32), my_cos, my_sin)[:, 0].astype(
        jnp.bfloat16
    )
    local_kv = jnp.concatenate([key_rot, head_kv[:, HEAD_DIMENSION:]], axis=1)
    key_value = lax.all_gather(local_kv, "ctx", axis=0, tiled=True)
    grad_query, grad_key, grad_value = attend(
        query_rot,
        upstream.reshape(tok_rows, head_count, HEAD_DIMENSION),
        key_value[:, :HEAD_DIMENSION],
        key_value[:, HEAD_DIMENSION:],
        my_pos,
        my_doc,
        positions,
        doc_all,
        HEAD_DIMENSION ** (-0.5),
    )
    query_back = (
        rotate_back(grad_query, my_cos, my_sin).astype(jnp.bfloat16).reshape(tok_rows, query_cols)
    )
    key_backward = rotate_back(grad_key[:, None, :], cosine_all, sine_all)[:, 0]
    key_terms = jnp.concatenate([key_backward, grad_value], axis=1)
    head_grad = lax.psum_scatter(
        key_terms.astype(jnp.bfloat16), "ctx", scatter_dimension=0, tiled=True
    ).astype(jnp.float32)
    for bit_index in reversed(range(pairing_flags)):
        half_width = head_grad.shape[1] // 2
        lower_half = head_grad[:, :half_width]
        upper_half = head_grad[:, half_width:]
        is_lower = tp_rank // (1 << bit_index) % 2 == 0
        retained = jnp.where(is_lower, lower_half, upper_half)
        outgoing = jnp.where(is_lower, upper_half, lower_half)
        head_grad = retained + partner_2(outgoing.astype(jnp.bfloat16), "tp", bit_index).astype(
            outgoing.dtype
        )
    key_value_backward = head_grad.astype(jnp.bfloat16)
    row_grads = jnp.concatenate([query_back, key_value_backward], axis=1)
    part_query = lax.dot_general(
        row_grads[:, :query_cols], query_full, (((1,), (1,)), ((), ())), preferred_element_type=f32
    )
    part_keyval = lax.dot_general(
        row_grads[:, query_cols:], keyval_full, (((1,), (1,)), ((), ())), preferred_element_type=f32
    )
    token_grad = lax.psum_scatter(
        (part_query + part_keyval).astype(jnp.bfloat16), "tp", scatter_dimension=0, tiled=True
    )
    weight_grad = lax.psum_scatter(
        lax.dot_general(
            gathered, row_grads, (((0,), (0,)), ((), ())), preferred_element_type=f32
        ).astype(jnp.bfloat16),
        "ctx",
        scatter_dimension=0,
        tiled=True,
    ).astype(jnp.float32)
    return (token_grad, weight_grad[:, :query_cols], weight_grad[:, query_cols:])


def solution(mesh):
    return jax.shard_map(
        shards,
        mesh=mesh,
        in_specs=(P(("ctx", "tp"), None), P("ctx", "tp"), P("ctx", "tp"), P("ctx", "tp"), P(), P()),
        out_specs=(P(("ctx", "tp"), None), P("ctx", "tp"), P("ctx", "tp")),
        check_vma=False,
    )
```

profile of v0, /device:TPU:0, one launch (start us, length us, event | category | flops | bytes accessed | tf_op | source)
XLA Modules:
  0.0 420.0 jit_solution(7259557244311544028)
XLA Ops:
  10.2 11.8 %gather_fusion = s32[2048]{0:T(1024)S(1)} fusion(s32[2048]{0:T(1024)S(1)} %copy-done, s32[2048]{0:T(1024)S(1)} %fusion.52), kind=kCustom, calls=%fused_computation | custom fusion | bytes 24576 | tf_op jit(solution)/shard_map/jit(_take)/gather | solution.py:104
  22.0 1.9 multiply_cosine_fusion
  23.9 23.9 %all-gather.9.cloned.1.call-done = bf16[4096,256]{1,0:T(8,128)(2,1)} async-done(((bf16[1024,256]{1,0:T(8,128)(2,1)}), bf16[4096,256]{1,0:T(8,128)(2,1)}) %all-gather.9.cloned.1.call-update) | async-done | bytes 2097168 | tf_op jit(solution)/shard_map/all_gather | solution.py:113
  47.8 48.5 %all-gather.5.cloned.1.call-done = bf16[512,4096]{1,0:T(8,128)(2,1)} async-done(((bf16[64,4096]{1,0:T(8,128)(2,1)}), bf16[512,4096]{1,0:T(8,128)(2,1)}) %all-gather.5.cloned.1.call-update) | async-done | bytes 4194320 | tf_op jit(solution)/shard_map/all_gather | solution.py:99
  96.3 4.2 convolution_convert_fusion.1
  105.0 44.5 %all-gather.7.cloned.1.call-done = bf16[4096,512]{1,0:T(8,128)(2,1)} async-done(((bf16[1024,512]{1,0:T(8,128)(2,1)}), bf16[4096,512]{1,0:T(8,128)(2,1)}) %all-gather.7.cloned.1.call-update) | async-done | bytes 4194320 | tf_op jit(solution)/shard_map/all_gather | solution.py:112
  149.6 5.8 %fusion.60 = f32[512,512]{0,1:T(8,128)S(1)} fusion(bf16[512,4096]{1,0:T(8,128)(2,1)} %all-gather.5.cloned.1.call-done, bf16[4096,512]{1,0:T(8,128)(2,1)} %all-gather.7.cloned.1.call-done), kind=kOutput, calls=%fused_computation.102 | convolution fusion | flops 2147483648 | bytes 9437184 | tf_op jit(solution)/shard_map/dot_general | solution.py:115
  156.3 1.5 fusion.42
  158.1 19.5 %all-gather.11.cloned.1.call-done = bf16[2048,256]{0,1:T(8,128)(2,1)} async-done(((bf16[512,256]{0,1:T(8,128)(2,1)}), bf16[2048,256]{0,1:T(8,128)(2,1)}) %all-gather.11.cloned.1.call-update) | async-done | bytes 1048592 | tf_op jit(solution)/shard_map/all_gather | solution.py:133
  177.7 2.1 fusion.58
  180.0 63.6 %while.15 = (s32[]{:T(128)}, f32[2048,128]{1,0:T(8,128)}, f32[2048,128]{1,0:T(8,128)}, f32[4,128,4,128]{3,1,2,0:T(8,128)}, s32[2048]{0:T(1024)S(1)}, /*index=5*/...) while((s32[]{:T(128)}, f32[2048,128]{1,0:T(8,128)}, ...), condition=%wide.region_4.5_spmd.clone, body=%wide.region_0.4_spmd.clone.sunk | while | flops 1625556480 | bytes 52066004 | solution.py:90
  181.9 1.9 fusion.106
  184.5 1.0 constant_dynamic-slice_fusion.4
  186.2 2.1 fusion.109
  188.3 3.5 fusion.110
  191.8 1.4 fusion.112
  193.2 1.8 fusion.111
  196.6 1.9 fusion.106
  200.9 2.1 fusion.109
  203.0 3.7 fusion.110
  206.8 1.4 fusion.112
  208.2 3.0 fusion.111
  212.9 1.9 fusion.106
  217.2 2.1 fusion.109
  219.3 3.7 fusion.110
  223.0 1.4 fusion.112
  224.4 3.0 fusion.111
  229.1 1.9 fusion.106
  233.4 2.1 fusion.109
  235.5 3.7 fusion.110
  239.2 1.4 fusion.112
  240.6 3.0 fusion.111
  243.6 1.6 copy.39
  245.2 1.4 fusion.35
  247.5 2.3 copy.41
  249.8 1.3 fusion.38
  251.1 2.2 pad_maximum_fusion.2
  255.3 26.1 %reduce-scatter.4.cloned.1.call-done = bf16[512,256]{0,1:T(8,128)(2,1)} async-done(((bf16[2048,256]{0,1:T(8,128)(2,1)}), bf16[512,256]{0,1:T(8,128)(2,1)}) %reduce-scatter.4.cloned.1.call-update) | async-done | bytes 262160 | tf_op jit(solution)/shard_map/reduce_scatter | solution.py:150
  281.4 1.1 copy.42
  282.5 7.6 %fusion.33 = bf16[4096,768]{0,1:T(8,128)(2,1)} fusion(bf16[512,4096]{1,0:T(8,128)(2,1)} %all-gather.5.cloned.1.call-done, bf16[512,256]{1,0:T(8,128)(2,1)S(1)} %copy.42, bf16[512,512]{1,0:T(8,128)(2,1)S(1)} %fusion.40), kind=kOutput, calls=%fused_computation.48 | convolution fusion | flops 3225944064 | bytes 11272192 | tf_op jit(solution)/shard_map/dot_general | solution.py:175
  290.4 4.7 %fusion.61 = f32[512,4096]{1,0:T(8,128)S(1)} fusion(bf16[512,512]{1,0:T(8,128)(2,1)S(1)} %fusion.40, bf16[4096,512]{1,0:T(8,128)(2,1)} %all-gather.7.cloned.1.call-done), kind=kOutput, calls=%fused_computation.103 | convolution fusion | flops 2147483648 | bytes 13107200 | tf_op jit(solution)/shard_map/dot_general | solution.py:165
  295.2 3.5 add_convert_fusion
  298.7 61.6 %reduce-scatter.8.cloned.1.call-done = bf16[1024,768]{0,1:T(8,128)(2,1)} async-done(((bf16[4096,768]{0,1:T(8,128)(2,1)}), bf16[1024,768]{0,1:T(8,128)(2,1)}) %reduce-scatter.8.cloned.1.call-update) | async-done | bytes 1572880 | tf_op jit(solution)/shard_map/reduce_scatter | solution.py:174
  360.3 1.5 slice.70
  361.8 1.8 copy.43
  363.6 1.1 slice.71
  364.8 1.3 copy.44
  366.1 47.1 %reduce-scatter.6.cloned.1.call-done = bf16[64,4096]{1,0:T(8,128)(2,1)} async-done(((bf16[512,4096]{1,0:T(8,128)(2,1)}), bf16[64,4096]{1,0:T(8,128)(2,1)}) %reduce-scatter.6.cloned.1.call-update) | async-done | bytes 524304 | tf_op jit(solution)/shard_map/reduce_scatter | solution.py:171
  (106 shorter events, 27.4 us)
Async XLA Ops:
  7.2 3.0 copy-start
  7.2 40.6 %all-gather.9.cloned.1.call-start = ((), (), s32[]{:S(2)}) async-start(), calls=%async_computation.5 | async-start | bytes 2621440 | tf_op jit(solution)/shard_map/all_gather | solution.py:113
  7.9 88.3 %all-gather.5.cloned.1.call-start = ((), (), s32[]{:S(2)}) async-start(), calls=%async_computation.3 | async-start | bytes 4718592 | tf_op jit(solution)/shard_map/all_gather | solution.py:99
  8.7 140.9 %all-gather.7.cloned.1.call-start = ((), (), s32[]{:S(2)}) async-start(), calls=%async_computation.4 | async-start | bytes 5242880 | tf_op jit(solution)/shard_map/all_gather | solution.py:112
  9.4 168.3 %all-gather.11.cloned.1.call-start = ((), (), s32[]{:S(2)}) async-start(), calls=%async_computation.6 | async-start | bytes 1310720 | tf_op jit(solution)/shard_map/all_gather | solution.py:133
  10.2 11.8 %copy-start.13 = (s32[2048]{0:T(1024)S(1)}, s32[2048]{0:T(1024)}, u32[]{:S(2)}) copy-start(s32[2048]{0:T(1024)} %param.12) | copy-start | bytes 24580
  23.9 76.6 %copy-start.3 = (f32[2048,64]{0,1:T(8,128)}, f32[2048,64]{0,1:T(8,128)S(1)}, u32[]{:S(2)}) copy-start(f32[2048,64]{0,1:T(8,128)S(1)} %get-tuple-element.183) | copy-start | bytes 1572868
  23.9 76.6 %copy-start.4 = (f32[2048,64]{0,1:T(8,128)}, f32[2048,64]{0,1:T(8,128)S(1)}, u32[]{:S(2)}) copy-start(f32[2048,64]{0,1:T(8,128)S(1)} %get-tuple-element.182) | copy-start | bytes 1572868
  100.4 1.0 copy-start.11
  101.4 180.0 %reduce-scatter.4.cloned.1.call-start = ((), (), s32[]{:S(2)}) async-start(), calls=%async_computation.7 | async-start | bytes 1310720 | tf_op jit(solution)/shard_map/reduce_scatter | solution.py:150
  104.2 45.4 %copy-start.7 = (f32[512,128]{1,0:T(8,128)}, f32[512,128]{1,0:T(8,128)S(1)}, u32[]{:S(2)}) copy-start(f32[512,128]{1,0:T(8,128)S(1)} %copy.29) | copy-start | bytes 786436
  183.8 1.6 copy-start.12
  188.3 3.5 copy-start.2
  198.5 1.6 copy-start.12
  203.0 3.7 copy-start.2
  214.8 1.6 copy-start.12
  219.3 3.7 copy-start.2
  231.0 1.6 copy-start.12
  235.5 3.7 copy-start.2
  243.6 6.2 %copy-start.5 = (f32[2048,64]{0,1:T(8,128)S(1)}, f32[2048,64]{0,1:T(8,128)}, u32[]{:S(2)}) copy-start(f32[2048,64]{0,1:T(8,128)} %copy-done.4) | copy-start | bytes 1572868
  247.5 5.9 %copy-start.6 = (f32[4,128,4,128]{3,1,2,0:T(8,128)S(1)}, f32[4,128,4,128]{3,1,2,0:T(8,128)}, u32[]{:S(2)}) copy-start(f32[4,128,4,128]{3,1,2,0:T(8,128)} %get-tuple-element.67) | copy-start | bytes 3145732
  251.1 3.1 copy-start.8
  253.3 107.0 %reduce-scatter.8.cloned.1.call-start = ((), (), s32[]{:S(2)}) async-start(), calls=%async_computation.9 | async-start | bytes 7864320 | tf_op jit(solution)/shard_map/reduce_scatter | solution.py:174
  290.2 5.0 %copy-start.9 = (bf16[4096,256]{1,0:T(8,128)(2,1)S(1)}, bf16[4096,256]{1,0:T(8,128)(2,1)}, u32[]{:S(2)}) copy-start(bf16[4096,256]{1,0:T(8,128)(2,1)} %all-gather.9.cloned.1.call-done) | copy-start | bytes 6291460
  290.2 5.0 %copy-start.10 = (bf16[512,256]{0,1:T(8,128)(2,1)S(1)}, bf16[512,256]{0,1:T(8,128)(2,1)}, u32[]{:S(2)}) copy-start(bf16[512,256]{0,1:T(8,128)(2,1)} %reduce-scatter.4.cloned.1.call-done) | copy-start | bytes 786436
  290.2 123.0 %reduce-scatter.6.cloned.1.call-start = ((), (), s32[]{:S(2)}) async-start(), calls=%async_computation.8 | async-start | bytes 4718592 | tf_op jit(solution)/shard_map/reduce_scatter | solution.py:171
  360.3 52.8 %copy-start.1 = (s32[2048]{0:T(1024)S(1)}, s32[2048]{0:T(1024)}, u32[]{:S(2)}) copy-start(s32[2048]{0:T(1024)} %param.13) | copy-start | bytes 24580
Sparse Core Ops, SparseCore 0:
  9.8 37.8 all-gather.8
  49.4 46.8 all-gather.4
  98.1 51.4 all-gather.6
  151.3 26.3 all-gather.10
  253.5 27.9 reduce-scatter.3
  290.3 70.0 reduce-scatter.7
  363.2 49.9 reduce-scatter.5
where the time goes:
time: 421 us; the launch traced here: 420 us
  waiting for transfers between devices  273 us (65%)
  matrix products  71.2 us (17%)
  local copies, waits for them, and re-layouts  37.1 us (9%)
  other arithmetic  23 us (5%)
  between operations  14.5 us (3%)
    reduce_scatter x1, waiting for transfers between devices, shards(): lax.psum_scatter(lax.dot_general(gathered, row_grads, (((0,), (0,)), ((),...  61.6 us
    all_gather x1, waiting for transfers between devices, shards(): gathered = lax.all_gather(tokens, 'tp', axis=0, tiled=True)  48.5 us
    reduce_scatter x1, waiting for transfers between devices, shards(): lax.psum_scatter((part_query + part_keyval).astype(jnp.bfloat16), 'tp', s...  47.1 us
    all_gather x1, waiting for transfers between devices, shards(): lax.all_gather(w_query, 'ctx', axis=0, tiled=True)  44.5 us
    reduce_scatter x1, waiting for transfers between devices, shards(): lax.psum_scatter(key_terms.astype(jnp.bfloat16), 'ctx', scatter_dimension...  26.1 us
    all_gather x1, waiting for transfers between devices, shards(): lax.all_gather(w_keyval, 'ctx', axis=0, tiled=True)  23.9 us
    all_gather x1, waiting for transfers between devices, shards(): key_value = lax.all_gather(local_kv, 'ctx', axis=0, tiled=True)  19.5 us
    dot_general x4, matrix products, advance(): jnp.einsum('hqk,qhd->kd', score_grad, query_block, preferred_element_type...  14.6 us
  transfers between devices with their start and end apart: 7, of which 7 were waited for; matrix products, arithmetic and copies ran while one was open for 11% of the time, Pallas kernels for 0%

commit v1 on v0

--- a/solution.py
+++ b/solution.py
@@ -96,7 +96,12 @@
     ctx_rank = lax.axis_index("ctx")
     tp_rank = lax.axis_index("tp")
     tensor_split_count = lax.axis_size("tp")
-    gathered = lax.all_gather(tokens, "tp", axis=0, tiled=True)
+    ring = [tokens]
+    for hop in range(7):
+        ring.append(lax.ppermute(ring[-1], "tp", [(dev, (dev + 1) % 8) for dev in range(8)]))
+    gathered = jnp.roll(
+        jnp.concatenate(ring[::-1], axis=0), (lax.axis_index("tp") + 1) * ring[0].shape[0], axis=0
+    )
     tok_rows = gathered.shape[0]
     query_cols = w_query.shape[1]
     head_count = query_cols // HEAD_DIMENSION

time: 421 us -> 440 us (1.045)
  local copies, waits for them, and re-layouts: 37.1 us -> 55.2 us
    ppermute x0 -> x7, waiting for transfers between devices: none -> 61.5 us  [shards(): lax.ppermute(ring[-1], 'tp', [(dev, (dev + 1) % 8) for dev in range(8)])]
    all_gather x1 -> x0, waiting for transfers between devices: 48.5 us -> none  [shards(): gathered = lax.all_gather(tokens, 'tp', axis=0, tiled=True)]
    all_gather x1, waiting for transfers between devices: 23.9 us -> 0.01 us  [shards(): lax.all_gather(w_keyval, 'ctx', axis=0, tiled=True)]
    unnamed x28 -> x49, local copies, waits for them, and re-layouts: 3.84 us -> 18.6 us
    all_gather x1, waiting for transfers between devices: 44.5 us -> 52.1 us  [shards(): lax.all_gather(w_query, 'ctx', axis=0, tiled=True)]
  transfers between devices with their start and end apart: 7 -> 13, of which waited for: 7 -> 11; matrix products, arithmetic and copies ran while one was open for 11% -> 12% of each run, Pallas kernels for 0% -> 0%
where the time goes in v1:
time: 440 us; the launch traced here: 438 us
  waiting for transfers between devices  272 us (62%)
  matrix products  72 us (16%)
  local copies, waits for them, and re-layouts  55.2 us (13%)
  other arithmetic  23.8 us (5%)
  between operations  14.5 us (3%)
    reduce_scatter x1, waiting for transfers between devices, shards(): lax.psum_scatter(lax.dot_general(gathered, row_grads, (((0,), (0,)), ((),...  61.8 us
    ppermute x7, waiting for transfers between devices, shards(): lax.ppermute(ring[-1], 'tp', [(dev, (dev + 1) % 8) for dev in range(8)])  61.5 us
    all_gather x1, waiting for transfers between devices, shards(): lax.all_gather(w_query, 'ctx', axis=0, tiled=True)  52.1 us
    reduce_scatter x1, waiting for transfers between devices, shards(): lax.psum_scatter((part_query + part_keyval).astype(jnp.bfloat16), 'tp', s...  48.7 us
    reduce_scatter x1, waiting for transfers between devices, shards(): lax.psum_scatter(key_terms.astype(jnp.bfloat16), 'ctx', scatter_dimension...  25.9 us
    all_gather x1, waiting for transfers between devices, shards(): key_value = lax.all_gather(local_kv, 'ctx', axis=0, tiled=True)  20.9 us
    unnamed x49, local copies, waits for them, and re-layouts  18.6 us
    dot_general x4, matrix products, advance(): jnp.einsum('hqk,qhd->kd', score_grad, query_block, preferred_element_type...  14.6 us
  transfers between devices with their start and end apart: 13, of which 11 were waited for; matrix products, arithmetic and copies ran while one was open for 12% of the time, Pallas kernels for 0%

profile of v1, /device:TPU:0, one launch (start us, length us, event | category | flops | bytes accessed | tf_op | source)
XLA Modules:
  0.0 438.5 jit_solution(3136624606851854081)
XLA Ops:
  7.8 11.1 %collective-permute-done = bf16[64,4096]{1,0:T(8,128)(2,1)S(1)} collective-permute-done((bf16[64,4096]{1,0:T(8,128)(2,1)}, bf16[64,4096]{1,0:T(8,128)(2,1)S(1)}, u32[]{:S(2)}, u32[]{:S(2)}) %collective-permute-start) | collective-permute-done | bytes 524320 | tf_op jit(solution)/shard_map/ppermute | solution.py:101
  18.9 10.4 %collective-permute-done.1 = bf16[64,4096]{1,0:T(8,128)(2,1)S(1)} collective-permute-done((bf16[64,4096]{1,0:T(8,128)(2,1)S(1)}, bf16[64,4096]{1,0:T(8,128)(2,1)S(1)}, u32[]{:S(2)}, u32[]{:S(2)}) %collective-permute-start.1) | collective-permute-done | bytes 524320 | tf_op jit(solution)/shard_map/ppermute | solution.py:101
  29.3 10.4 %collective-permute-done.2 = bf16[64,4096]{1,0:T(8,128)(2,1)S(1)} collective-permute-done((bf16[64,4096]{1,0:T(8,128)(2,1)S(1)}, bf16[64,4096]{1,0:T(8,128)(2,1)S(1)}, u32[]{:S(2)}, u32[]{:S(2)}) %collective-permute-start.2) | collective-permute-done | bytes 524320 | tf_op jit(solution)/shard_map/ppermute | solution.py:101
  39.7 10.4 %collective-permute-done.3 = bf16[64,4096]{1,0:T(8,128)(2,1)S(1)} collective-permute-done((bf16[64,4096]{1,0:T(8,128)(2,1)S(1)}, bf16[64,4096]{1,0:T(8,128)(2,1)S(1)}, u32[]{:S(2)}, u32[]{:S(2)}) %collective-permute-start.3) | collective-permute-done | bytes 524320 | tf_op jit(solution)/shard_map/ppermute | solution.py:101
  50.1 10.4 %collective-permute-done.4 = bf16[64,4096]{1,0:T(8,128)(2,1)S(1)} collective-permute-done((bf16[64,4096]{1,0:T(8,128)(2,1)S(1)}, bf16[64,4096]{1,0:T(8,128)(2,1)S(1)}, u32[]{:S(2)}, u32[]{:S(2)}) %collective-permute-start.4) | collective-permute-done | bytes 524320 | tf_op jit(solution)/shard_map/ppermute | solution.py:101
  61.3 11.8 %gather_fusion = s32[2048]{0:T(1024)S(1)} fusion(s32[2048]{0:T(1024)S(1)} %copy-done, s32[2048]{0:T(1024)S(1)} %fusion.59), kind=kCustom, calls=%fused_computation | custom fusion | bytes 24576 | tf_op jit(solution)/shard_map/jit(_take)/gather | solution.py:109
  73.3 1.9 multiply_cosine_fusion
  75.2 8.7 %collective-permute-done.6 = bf16[64,4096]{1,0:T(8,128)(2,1)} collective-permute-done((bf16[64,4096]{1,0:T(8,128)(2,1)}, bf16[64,4096]{1,0:T(8,128)(2,1)}, u32[]{:S(2)}, u32[]{:S(2)}) %collective-permute-start.6) | collective-permute-done | bytes 524320 | tf_op jit(solution)/shard_map/ppermute | solution.py:101
  83.9 1.9 constant_dynamic-update-slice_fusion.15
  85.8 1.9 constant_dynamic-update-slice_fusion.14
  87.7 1.9 constant_dynamic-update-slice_fusion.13
  93.8 1.9 constant_dynamic-update-slice_fusion.7
  95.7 1.9 constant_dynamic-update-slice_fusion.6
  102.7 4.2 fusion.38
  112.1 20.9 %all-gather.8.cloned.1.call-done = bf16[2048,256]{0,1:T(8,128)(2,1)} async-done(((bf16[512,256]{0,1:T(8,128)(2,1)}), bf16[2048,256]{0,1:T(8,128)(2,1)}) %all-gather.8.cloned.1.call-update) | async-done | bytes 1048592 | tf_op jit(solution)/shard_map/all_gather | solution.py:138
  133.0 2.1 fusion.68
  135.4 52.1 %all-gather.4.cloned.1.call-done = bf16[4096,512]{1,0:T(8,128)(2,1)} async-done(((bf16[1024,512]{1,0:T(8,128)(2,1)}), bf16[4096,512]{1,0:T(8,128)(2,1)}) %all-gather.4.cloned.1.call-update) | async-done | bytes 4194320 | tf_op jit(solution)/shard_map/all_gather | solution.py:117
  187.4 5.8 %fusion.36 = f32[512,512]{0,1:T(8,128)S(1)} fusion(bf16[4096,512]{1,0:T(8,128)(2,1)} %all-gather.4.cloned.1.call-done, bf16[1024,4096]{1,0:T(8,128)(2,1)} %constant_dynamic-update-slice_fusion, s32[]{:T(128)S(6)} %select_n.39), kind=kOutput, calls=%fused_computation.51 | convolution fusion | flops 2147483648 | bytes 9437188 | tf_op jit(solution)/shard_map/dot_general | solution.py:120
  196.0 1.5 fusion.49
  197.8 63.7 %while.15 = (s32[]{:T(128)}, f32[2048,128]{1,0:T(8,128)}, f32[2048,128]{1,0:T(8,128)}, f32[4,128,4,128]{3,1,2,0:T(8,128)}, s32[2048]{0:T(1024)S(1)}, /*index=5*/...) while((s32[]{:T(128)}, f32[2048,128]{1,0:T(8,128)}, ...), condition=%wide.region_4.5_spmd.clone, body=%wide.region_0.4_spmd.clone.sunk | while | flops 1625556480 | bytes 52066004 | solution.py:90
  199.7 1.9 fusion.112
  204.0 2.1 fusion.115
  206.1 3.5 fusion.116
  211.0 1.8 fusion.117
  214.5 1.9 fusion.112
  218.8 2.1 fusion.115
  220.9 3.7 fusion.116
  224.6 1.4 fusion.118
  226.0 3.0 fusion.117
  230.7 1.9 fusion.112
  235.0 2.1 fusion.115
  237.1 3.7 fusion.116
  242.2 3.0 fusion.117
  246.9 1.9 fusion.112
  251.2 2.1 fusion.115
  253.3 3.7 fusion.116
  257.1 1.4 fusion.118
  258.5 3.0 fusion.117
  261.5 1.6 copy.37
  265.4 2.3 copy.39
  269.0 2.2 pad_maximum_fusion.2
  273.4 25.9 %reduce-scatter.4.cloned.1.call-done = bf16[512,256]{0,1:T(8,128)(2,1)} async-done(((bf16[2048,256]{0,1:T(8,128)(2,1)}), bf16[512,256]{0,1:T(8,128)(2,1)}) %reduce-scatter.4.cloned.1.call-update) | async-done | bytes 262160 | tf_op jit(solution)/shard_map/reduce_scatter | solution.py:155
  300.4 8.4 %convolution_convert_fusion = bf16[4096,768]{1,0:T(8,128)(2,1)} fusion(bf16[1024,4096]{1,0:T(8,128)(2,1)} %constant_dynamic-update-slice_fusion, s32[]{:T(128)S(6)} %select_n.39, bf16[512,256]{1,0:T(8,128)(2,1)S(1)} %copy.40, bf16[512,512]{1,0:T(8,128)(2,1)S(1)} %fusion.47), kind=kOutput, calls=%fused_computation.47 | convolution fusion | flops 3225944064 | bytes 11272196 | tf_op jit(solution)/shard_map/dot_general | solution.py:180
  308.9 4.7 %fusion.70 = f32[512,4096]{1,0:T(8,128)S(1)} fusion(bf16[512,512]{1,0:T(8,128)(2,1)S(1)} %fusion.47, bf16[4096,512]{1,0:T(8,128)(2,1)} %all-gather.4.cloned.1.call-done), kind=kOutput, calls=%fused_computation.125 | convolution fusion | flops 2147483648 | bytes 13107200 | tf_op jit(solution)/shard_map/dot_general | solution.py:170
  313.6 3.5 add_convert_fusion
  317.1 61.8 %reduce-scatter.8.cloned.1.call-done = bf16[1024,768]{1,0:T(8,128)(2,1)} async-done(((bf16[4096,768]{1,0:T(8,128)(2,1)}), bf16[1024,768]{1,0:T(8,128)(2,1)}) %reduce-scatter.8.cloned.1.call-update) | async-done | bytes 1572880 | tf_op jit(solution)/shard_map/reduce_scatter | solution.py:179
  379.0 3.0 slice.70
  383.0 48.7 %reduce-scatter.6.cloned.1.call-done = bf16[64,4096]{1,0:T(8,128)(2,1)} async-done(((bf16[512,4096]{1,0:T(8,128)(2,1)}), bf16[64,4096]{1,0:T(8,128)(2,1)}) %reduce-scatter.6.cloned.1.call-update) | async-done | bytes 524304 | tf_op jit(solution)/shard_map/reduce_scatter | solution.py:176
  (139 shorter events, 46.3 us)
Async XLA Ops:
  7.2 54.1 %copy-start = (s32[2048]{0:T(1024)S(1)}, s32[2048]{0:T(1024)}, u32[]{:S(2)}) copy-start(s32[2048]{0:T(1024)} %param.13) | copy-start | bytes 24580
  7.2 95.5 %all-gather.6.cloned.1.call-start = ((), (), s32[]{:S(2)}) async-start(), calls=%async_computation.4 | async-start | bytes 2621440 | tf_op jit(solution)/shard_map/all_gather | solution.py:118
  7.2 11.6 %collective-permute-start = (bf16[64,4096]{1,0:T(8,128)(2,1)}, bf16[64,4096]{1,0:T(8,128)(2,1)S(1)}, u32[]{:S(2)}, u32[]{:S(2)}) collective-permute-start(bf16[64,4096]{1,0:T(8,128)(2,1)} %param.8), channel_id=1, source_target_pairs={{0,1},{1,2},{2,3},{3,4},{4,5},{5,6},{6,7},{7,0},{8,9},{9,10},{10,1... | collective-permute-start | bytes 1572872 | tf_op jit(solution)/shard_map/ppermute | solution.py:101
  18.9 10.4 %collective-permute-start.1 = (bf16[64,4096]{1,0:T(8,128)(2,1)S(1)}, bf16[64,4096]{1,0:T(8,128)(2,1)S(1)}, u32[]{:S(2)}, u32[]{:S(2)}) collective-permute-start(bf16[64,4096]{1,0:T(8,128)(2,1)S(1)} %collective-permute-done), channel_id=1, source_target_pairs={{0,1},{1,2},{2,3},{3,4},{4,5},{5,6},{6,7},{7,0},{8,9},{9,10},{10,1... | collective-permute-start | bytes 1572872 | tf_op jit(solution)/shard_map/ppermute | solution.py:101
  29.3 10.4 %collective-permute-start.2 = (bf16[64,4096]{1,0:T(8,128)(2,1)S(1)}, bf16[64,4096]{1,0:T(8,128)(2,1)S(1)}, u32[]{:S(2)}, u32[]{:S(2)}) collective-permute-start(bf16[64,4096]{1,0:T(8,128)(2,1)S(1)} %collective-permute-done.1), channel_id=1, source_target_pairs={{0,1},{1,2},{2,3},{3,4},{4,5},{5,6},{6,7},{7,0},{8,9},{9,10},{10,1... | collective-permute-start | bytes 1572872 | tf_op jit(solution)/shard_map/ppermute | solution.py:101
  39.7 10.4 %collective-permute-start.3 = (bf16[64,4096]{1,0:T(8,128)(2,1)S(1)}, bf16[64,4096]{1,0:T(8,128)(2,1)S(1)}, u32[]{:S(2)}, u32[]{:S(2)}) collective-permute-start(bf16[64,4096]{1,0:T(8,128)(2,1)S(1)} %collective-permute-done.2), channel_id=1, source_target_pairs={{0,1},{1,2},{2,3},{3,4},{4,5},{5,6},{6,7},{7,0},{8,9},{9,10},{10,1... | collective-permute-start | bytes 1572872 | tf_op jit(solution)/shard_map/ppermute | solution.py:101
  50.1 10.4 %collective-permute-start.4 = (bf16[64,4096]{1,0:T(8,128)(2,1)S(1)}, bf16[64,4096]{1,0:T(8,128)(2,1)S(1)}, u32[]{:S(2)}, u32[]{:S(2)}) collective-permute-start(bf16[64,4096]{1,0:T(8,128)(2,1)S(1)} %collective-permute-done.3), channel_id=1, source_target_pairs={{0,1},{1,2},{2,3},{3,4},{4,5},{5,6},{6,7},{7,0},{8,9},{9,10},{10,1... | collective-permute-start | bytes 1572872 | tf_op jit(solution)/shard_map/ppermute | solution.py:101
  60.5 12.6 %copy-start.12 = (bf16[64,4096]{1,0:T(8,128)(2,1)}, bf16[64,4096]{1,0:T(8,128)(2,1)S(1)}, u32[]{:S(2)}) copy-start(bf16[64,4096]{1,0:T(8,128)(2,1)S(1)} %collective-permute-done.4) | copy-start | bytes 1572868
  60.5 12.6 %collective-permute-start.5 = (bf16[64,4096]{1,0:T(8,128)(2,1)S(1)}, bf16[64,4096]{1,0:T(8,128)(2,1)}, u32[]{:S(2)}, u32[]{:S(2)}) collective-permute-start(bf16[64,4096]{1,0:T(8,128)(2,1)S(1)} %collective-permute-done.4), channel_id=1, source_target_pairs={{0,1},{1,2},{2,3},{3,4},{4,5},{5,6},{6,7},{7,0},{8,9},{9,10},{10,1... | collective-permute-start | bytes 1572872 | tf_op jit(solution)/shard_map/ppermute | solution.py:101
  60.5 72.5 %all-gather.8.cloned.1.call-start = ((), (), s32[]{:S(2)}) async-start(), calls=%async_computation.5 | async-start | bytes 1310720 | tf_op jit(solution)/shard_map/all_gather | solution.py:138
  61.3 11.8 %copy-start.17 = (s32[2048]{0:T(1024)S(1)}, s32[2048]{0:T(1024)}, u32[]{:S(2)}) copy-start(s32[2048]{0:T(1024)} %param.12) | copy-start | bytes 24580
  73.1 10.8 %collective-permute-start.6 = (bf16[64,4096]{1,0:T(8,128)(2,1)}, bf16[64,4096]{1,0:T(8,128)(2,1)}, u32[]{:S(2)}, u32[]{:S(2)}) collective-permute-start(bf16[64,4096]{1,0:T(8,128)(2,1)} %collective-permute-done.5), channel_id=1, source_target_pairs={{0,1},{1,2},{2,3},{3,4},{4,5},{5,6},{6,7},{7,0},{8,9},{9,10},{10,1... | collective-permute-start | bytes 1572872 | tf_op jit(solution)/shard_map/ppermute | solution.py:101
  73.3 19.7 %copy-start.11 = (bf16[64,4096]{1,0:T(8,128)(2,1)S(1)}, bf16[64,4096]{1,0:T(8,128)(2,1)}, u32[]{:S(2)}) copy-start(bf16[64,4096]{1,0:T(8,128)(2,1)} %param.8) | copy-start | bytes 1572868
  75.2 31.8 %copy-start.4 = (f32[2048,64]{0,1:T(8,128)}, f32[2048,64]{0,1:T(8,128)S(1)}, u32[]{:S(2)}) copy-start(f32[2048,64]{0,1:T(8,128)S(1)} %get-tuple-element.177) | copy-start | bytes 1572868
  75.2 31.8 %copy-start.5 = (f32[2048,64]{0,1:T(8,128)}, f32[2048,64]{0,1:T(8,128)S(1)}, u32[]{:S(2)}) copy-start(f32[2048,64]{0,1:T(8,128)S(1)} %get-tuple-element.176) | copy-start | bytes 1572868
  87.7 9.9 %copy-start.13 = (bf16[64,4096]{1,0:T(8,128)(2,1)S(1)}, bf16[64,4096]{1,0:T(8,128)(2,1)}, u32[]{:S(2)}) copy-start(bf16[64,4096]{1,0:T(8,128)(2,1)} %copy-done.12) | copy-start | bytes 1572868
  106.8 1.8 copy-start.15
  107.8 79.7 %all-gather.4.cloned.1.call-start = ((), (), s32[]{:S(2)}) async-start(), calls=%async_computation.3 | async-start | bytes 5242880 | tf_op jit(solution)/shard_map/all_gather | solution.py:117
  108.5 190.8 %reduce-scatter.4.cloned.1.call-start = ((), (), s32[]{:S(2)}) async-start(), calls=%async_computation.6 | async-start | bytes 1310720 | tf_op jit(solution)/shard_map/reduce_scatter | solution.py:155
  111.3 23.8 %copy-start.8 = (f32[512,128]{1,0:T(8,128)}, f32[512,128]{1,0:T(8,128)S(1)}, u32[]{:S(2)}) copy-start(f32[512,128]{1,0:T(8,128)S(1)} %copy.27) | copy-start | bytes 786436
  201.6 1.6 copy-start.16
  206.1 3.5 copy-start.2
  216.3 1.6 copy-start.16
  220.9 3.7 copy-start.2
  232.6 1.6 copy-start.16
  237.1 3.7 copy-start.2
  248.8 1.6 copy-start.16
  253.3 3.7 copy-start.2
  261.5 6.2 %copy-start.6 = (f32[2048,64]{0,1:T(8,128)S(1)}, f32[2048,64]{0,1:T(8,128)}, u32[]{:S(2)}) copy-start(f32[2048,64]{0,1:T(8,128)} %copy-done.5) | copy-start | bytes 1572868
  265.4 6.1 %copy-start.7 = (f32[4,128,4,128]{3,1,2,0:T(8,128)S(1)}, f32[4,128,4,128]{3,1,2,0:T(8,128)}, u32[]{:S(2)}) copy-start(f32[4,128,4,128]{3,1,2,0:T(8,128)} %get-tuple-element.67) | copy-start | bytes 3145732
  268.9 3.3 copy-start.9
  271.2 107.8 %reduce-scatter.8.cloned.1.call-start = ((), (), s32[]{:S(2)}) async-start(), calls=%async_computation.8 | async-start | bytes 7864320 | tf_op jit(solution)/shard_map/reduce_scatter | solution.py:179
  308.8 4.8 %copy-start.10 = (bf16[4096,256]{1,0:T(8,128)(2,1)S(1)}, bf16[4096,256]{1,0:T(8,128)(2,1)}, u32[]{:S(2)}) copy-start(bf16[4096,256]{1,0:T(8,128)(2,1)} %all-gather.6.cloned.1.call-done) | copy-start | bytes 6291460
  308.8 4.8 %copy-start.14 = (bf16[512,256]{0,1:T(8,128)(2,1)S(1)}, bf16[512,256]{0,1:T(8,128)(2,1)}, u32[]{:S(2)}) copy-start(bf16[512,256]{0,1:T(8,128)(2,1)} %reduce-scatter.4.cloned.1.call-done) | copy-start | bytes 786436
  308.8 122.8 %reduce-scatter.6.cloned.1.call-start = ((), (), s32[]{:S(2)}) async-start(), calls=%async_computation.7 | async-start | bytes 4718592 | tf_op jit(solution)/shard_map/reduce_scatter | solution.py:176
  317.1 114.5 %copy-start.1 = (s32[2048]{0:T(1024)S(1)}, s32[2048]{0:T(1024)}, u32[]{:S(2)}) copy-start(s32[2048]{0:T(1024)} %param.13) | copy-start | bytes 24580
  379.0 3.0 copy-start.3
Sparse Core Ops, SparseCore 0:
  60.6 36.8 all-gather.5
  107.9 25.0 all-gather.7
  134.8 52.5 all-gather.3
  271.3 27.9 reduce-scatter.3
  308.9 70.0 reduce-scatter.7
  381.7 49.9 reduce-scatter.5
